TPU v7x, 32 devices: a whole 2x2x4 slice. The times are simulated.
32 devices in a mesh: grp: 2 (over y), dev: 16 (over z, x, core).
Axes of the slice: x: 2, y: 2, z: 4, core: 2. Of those that a mesh axis runs over, the one named last changes fastest.
Arguments:
- pooled_grad: bfloat16 [4096, 32, 128], P(('grp', 'dev')), may hold values from -6 to 6
- row_ids: int32 [4096, 4, 32], P(('grp', 'dev')), may hold values from 0 to 1023
- scale_exps: int32 [4096, 32], P(('grp', 'dev')), may hold values from 0 to 3
- table_owner: int32 [32], replicated, may hold values from 0 to 31, each once
- dense_acts: bfloat16 [4096, 512], P(('grp', 'dev')), may hold values from -6 to 6
- dense_cot: bfloat16 [4096, 512], P(('grp', 'dev')), may hold values from -0.1875 to 0.1875
Outputs:
- table_grad: float32 [32, 1024, 128], P('dev')
- weight_grad: float32 [512, 512], replicated
- bias_grad: float32 [512], replicated
Inputs may be any that keep to these rules, and one draw needn't show every extreme that they name: Table t's rows are accumulated into slot table_owner[t]; each slot belongs to exactly one table.
All inputs are finite; a program needn't handle non-finite values.
Results may differ from a plain program's by a relative error of at most 0.0003.
Values may be sent and summed in bfloat16 or wider, within the bound.
A program may use at most 128 MiB of HBM per device.

v0:
```python
import math
import jax
import jax.numpy as jnp
from jax import lax
from jax.sharding import PartitionSpec as P

ROWS = 1024


def powers(exps):
    return (
        1.0
        + (exps >= 1).astype(jnp.float32)
        + 2.0 * (exps >= 2).astype(jnp.float32)
        + 4.0 * (exps >= 3).astype(jnp.float32)
    )


def accumulate(grads, indices, exps):
    samples = grads.shape[0]
    slots = grads.shape[2]
    pool_len = indices.shape[3]
    block_rows = math.gcd(samples, 1024)
    row_axis = lax.broadcasted_iota(jnp.int32, (ROWS, 1), 0)
    results = []
    for slot_pos in range(slots):
        factor = powers(exps[:, 0, slot_pos])
        restored = (grads[:, 0, slot_pos, :].astype(jnp.float32) * factor[:, None]).astype(
            jnp.bfloat16
        )
        row_index = indices[:, 0, slot_pos, :]

        def add_block(count, running, restored=restored, row_index=row_index):
            offset = count * block_rows
            values = lax.dynamic_slice_in_dim(restored, offset, block_rows, 0)
            picked = lax.dynamic_slice_in_dim(row_index, offset, block_rows, 0)
            counts = jnp.zeros((ROWS, block_rows), jnp.float32)
            for lookup in range(pool_len):
                counts = counts + (picked[:, lookup][None, :] == row_axis).astype(jnp.float32)
            return running + jnp.dot(
                counts.astype(jnp.bfloat16), values, preferred_element_type=jnp.float32
            )

        start_grad = jnp.zeros((ROWS, grads.shape[3]), jnp.float32)
        results.append(lax.fori_loop(0, samples // block_rows, add_block, start_grad))
    return jnp.stack(results, 0)


def per_device(pooled_grad, row_ids, scale_exps, table_owner, dense_acts, dense_cot):
    batch_rows, tables, feat_width = pooled_grad.shape
    dev_count = lax.axis_size("dev")
    per_owner = tables // dev_count
    pool_len = row_ids.shape[1]
    factor = powers(scale_exps)
    quantized = jnp.clip(pooled_grad.astype(jnp.float32) / factor[:, :, None], -1.0, 1.0).astype(
        jnp.bfloat16
    )
    slot_table = (
        jnp.zeros((tables,), jnp.int32).at[table_owner].set(jnp.arange(tables, dtype=jnp.int32))
    )
    send_grads = jnp.take(quantized, slot_table, axis=1).reshape(
        batch_rows, dev_count, per_owner, feat_width
    )
    send_rows = jnp.transpose(
        jnp.take(row_ids, slot_table, axis=2).reshape(batch_rows, pool_len, dev_count, per_owner),
        (0, 2, 3, 1),
    )
    send_exps = jnp.take(scale_exps, slot_table, axis=1).reshape(batch_rows, dev_count, per_owner)
    weight_term = lax.dot_general(
        dense_acts, dense_cot, (((0,), (0,)), ((), ())), preferred_element_type=jnp.float32
    )
    bias_term = jnp.sum(dense_cot.astype(jnp.float32), axis=0)
    partial_grad = accumulate(
        lax.all_to_all(send_grads, "dev", split_axis=1, concat_axis=0, tiled=True),
        lax.all_to_all(send_rows, "dev", split_axis=1, concat_axis=0, tiled=True),
        lax.all_to_all(send_exps, "dev", split_axis=1, concat_axis=0, tiled=True),
    )
    table_grad = lax.psum(partial_grad, "grp")
    dense_parts = (
        lax.psum_scatter(weight_term, "dev", scatter_dimension=0, tiled=True),
        lax.psum_scatter(bias_term, "dev", scatter_dimension=0, tiled=True),
    )
    dense_parts = lax.psum((dense_parts[0], dense_parts[1]), "grp")
    weight_grad, bias_grad = (
        lax.all_gather(dense_parts[0], "dev", axis=0, tiled=True),
        lax.all_gather(dense_parts[1], "dev", axis=0, tiled=True),
    )
    return (table_grad, weight_grad, bias_grad)


def solution(mesh):
    return jax.shard_map(
        per_device,
        mesh=mesh,
        in_specs=(
            P(("grp", "dev"), None, None),
            P(("grp", "dev"), None, None),
            P(("grp", "dev"), None),
            P(),
            P(("grp", "dev"), None),
            P(("grp", "dev"), None),
        ),
        out_specs=(P("dev", None, None), P(), P()),
        check_vma=False,
    )
```

profile of v0, /device:TPU:0, one launch (start us, length us, event | category | flops | bytes accessed | tf_op | source)
XLA Modules:
  0.0 227.3 jit_solution(12590961035273388617)
XLA Ops:
  7.2 0.0 copy-start
  7.2 0.0 copy-start.1
  7.2 0.7 compare_select_fusion.5
  7.9 0.7 scatter_custom_fusion
  8.6 0.1 broadcast_in_dim.41
  8.7 1.3 gather_fusion.2
  10.0 0.7 broadcast_select_fusion.1
  10.7 7.4 %all-to-all-start.2 = ((s32[128,16,2]{0,2,1:T(2,128)}), s32[128,16,2]{0,2,1:T(2,128)S(1)}, u32[]{:S(2)}, u32[]{:S(2)}) async-start(s32[128,16,2]{0,2,1:T(2,128)} %broadcast_select_fusion.1), calls=%async_computation.2 | async-start | bytes 32768 | tf_op jit(solution)/shard_map/all_to_all | solution.py:76
  18.1 0.7 select_add_fusion
  18.8 0.0 copy-done.1
  18.8 0.0 copy-start.2
  18.8 0.6 gather_fusion
  19.5 0.6 copy-done.2
  20.1 1.4 clamp_convert_fusion
  21.5 0.7 fusion.14
  22.2 0.7 gather_fusion.1
  22.9 1.7 all-to-all-done.2
  24.6 4.4 %all-to-all-start = ((s32[128,16,2,4]{0,2,3,1:T(2,128)}), s32[128,16,2,4]{0,2,3,1:T(2,128)S(1)}, u32[]{:S(2)}, u32[]{:S(2)}) async-start(s32[128,16,2,4]{0,2,3,1:T(2,128)} %fusion.14), calls=%async_computation | async-start | bytes 131072 | tf_op jit(solution)/shard_map/all_to_all | solution.py:75
  29.0 1.1 broadcast_select_fusion
  30.1 0.0 copy-start.4
  30.1 5.8 %all-to-all-done = s32[128,16,2,4]{0,2,3,1:T(2,128)S(1)} async-done(((s32[128,16,2,4]{0,2,3,1:T(2,128)}), s32[128,16,2,4]{0,2,3,1:T(2,128)S(1)}, u32[]{:S(2)}, u32[]{:S(2)}) %all-to-all-start) | async-done | bytes 65568 | tf_op jit(solution)/shard_map/all_to_all | solution.py:75
  35.9 3.7 %all-to-all-start.1 = ((bf16[128,16,2,128]{3,0,2,1:T(8,128)(2,1)}), bf16[128,16,2,128]{3,0,2,1:T(8,128)(2,1)S(1)}, u32[]{:S(2)}, u32[]{:S(2)}) async-start(bf16[128,16,2,128]{3,0,2,1:T(8,128)(2,1)} %broadcast_select_fusion), calls=%async_computation.1 | async-start | bytes 2097152 | tf_op jit(solution)/shard_map/all_to_all | solution.py:74
  39.5 0.0 reduce-scatter.2.cloned.1.call-start
  39.6 0.0 copy-done
  39.6 0.0 copy-done.4
  39.6 1.3 fusion.25
  40.9 0.0 reduce-scatter.2.cloned.1.call-update
  40.9 0.0 all-reduce.5.cloned.1.call-start
  41.1 21.3 %all-to-all-done.1 = bf16[128,16,2,128]{3,0,2,1:T(8,128)(2,1)S(1)} async-done(((bf16[128,16,2,128]{3,0,2,1:T(8,128)(2,1)}), bf16[128,16,2,128]{3,0,2,1:T(8,128)(2,1)S(1)}, u32[]{:S(2)}, u32[]{:S(2)}) %all-to-all-start.1) | async-done | bytes 1048608 | tf_op jit(solution)/shard_map/all_to_all | solution.py:74
  62.4 0.1 copy.26
  62.5 0.7 fusion.13
  63.2 4.5 %while.31 = (s32[]{:T(128)}, f32[1024,128]{1,0:T(8,128)S(1)}, s32[2048,4]{0,1:T(4,128)S(1)}, bf16[2048,128]{1,0:T(8,128)(2,1)S(1)}, s32[]{:T(128)}, /*index=5*/s...) while((s32[]{:T(128)}, f32[1024,128]{1,0:T(8,128)S(1)}, ...), condition=%wide.region_4.5_spmd.clone.clone, body=%wide.region_3.4_spmd.clone.clone.sunk | while | flops 281280512 | bytes 1360101 | solution.py:45
  63.2 0.1 constant_dynamic-slice_fusion.5
  63.4 2.1 fusion.35
  65.5 0.1 constant_dynamic-slice_fusion.5
  65.6 2.1 fusion.35
  67.7 4.5 %while.30 = (s32[]{:T(128)}, f32[1024,128]{1,0:T(8,128)S(1)}, s32[2048,4]{0,1:T(4,128)S(1)}, bf16[2048,128]{1,0:T(8,128)(2,1)S(1)}, s32[]{:T(128)}, /*index=5*/s...) while((s32[]{:T(128)}, f32[1024,128]{1,0:T(8,128)S(1)}, ...), condition=%wide.region_2.3_spmd.clone.clone, body=%wide.region_1.2_spmd.clone.clone.sunk | while | flops 281280512 | bytes 1360101 | solution.py:45
  67.7 0.1 constant_dynamic-slice_fusion.4
  67.8 2.1 fusion.33
  69.9 0.1 constant_dynamic-slice_fusion.4
  70.1 2.1 fusion.33
  72.2 1.0 pad_maximum_fusion
  73.2 0.0 copy-start.5
  73.2 30.2 %reduce-scatter.2.cloned.1.call-done = f32[32,512]{1,0:T(8,128)} async-done(((f32[512,512]{1,0:T(8,128)}), f32[32,512]{1,0:T(8,128)}) %reduce-scatter.2.cloned.1.call-update) | async-done | bytes 65552 | tf_op jit(solution)/shard_map/reduce_scatter | solution.py:80
  103.5 0.0 all-reduce.5.cloned.1.call-update
  103.5 0.0 all-gather.2.cloned.1.call-start
  103.5 43.6 %all-reduce.5.cloned.1.call-done = (f32[2,1024,128]{2,1,0:T(8,128)}, f32[32,512]{1,0:T(8,128)}) async-done(((f32[2,1024,128]{2,1,0:T(8,128)}, f32[32,512]{1,0:T(8,128)}), (f32[2,1024,128]{2,1,0:T(8,128)}, f32[32,512]{1,0:T(8,128)})) %all-reduce.5.cloned.1.call-update) | async-done | bytes 1114128 | tf_op jit(solution)/shard_map/psum | solution.py:78
  147.1 0.0 all-gather.2.cloned.1.call-update
  147.1 0.0 copy-done.5
  147.1 0.6 fusion.24
  148.4 33.2 %all-reduce.1 = f32[512]{0:T(512)S(1)} all-reduce(f32[512]{0:T(512)S(1)} %convert_reduce_fusion), channel_id=3, replica_groups=mesh['grp'=2,'dev'=16] {'dev'}, use_global_device_ids=true, to_apply=%region_9.10.clone | all-reduce | flops 512 | bytes 4096
  181.6 0.1 dynamic-slice.2
  182.3 4.9 %psum.23 = f32[32]{0:T(128)S(1)} all-reduce(f32[32]{0:T(128)S(1)} %dynamic-slice.2), channel_id=1, replica_groups=mesh['grp'=2,'dev'=16] {'grp'}, use_global_device_ids=true, to_apply=%region_10.11 | all-reduce | flops 32 | bytes 256 | tf_op jit(solution)/shard_map/psum | solution.py:83
  187.3 0.2 dynamic-update-slice
  187.4 30.0 %all-reduce = f32[512]{0:T(512)} all-reduce(f32[512]{0:T(512)S(1)} %dynamic-update-slice), channel_id=1, replica_groups=mesh['grp'=2,'dev'=16] {'dev'}, use_global_device_ids=true, to_apply=%add | all-reduce | flops 512 | bytes 4096
  217.5 0.0 all-gather.2.cloned.1.call-done
  217.5 0.0 copy-start.3
  217.5 2.4 %copy.52 = f32[2,1024,128]{2,1,0:T(8,128)} copy(f32[2,1024,128]{2,1,0:T(8,128)} %get-tuple-element.448) | data formatting | bytes 2097152
  219.8 0.0 copy-done.3
  219.8 1.0 copy.53
  (13 shorter events, 0.2 us)
Async XLA Ops:
  7.2 32.4 %copy-start = (bf16[128,512]{1,0:T(8,128)(2,1)S(1)}, bf16[128,512]{1,0:T(8,128)(2,1)}, u32[]{:S(2)}) copy-start(bf16[128,512]{1,0:T(8,128)(2,1)} %param.14) | copy-start | bytes 393220
  7.2 11.7 %copy-start.1 = (s32[128,4,32]{0,2,1:T(8,128)S(1)}, s32[128,4,32]{0,2,1:T(8,128)}, u32[]{:S(2)}) copy-start(s32[128,4,32]{0,2,1:T(8,128)} %param.11) | copy-start | bytes 196612
  10.7 13.9 %all-to-all-start.2 = ((s32[128,16,2]{0,2,1:T(2,128)}), s32[128,16,2]{0,2,1:T(2,128)S(1)}, u32[]{:S(2)}, u32[]{:S(2)}) async-start(s32[128,16,2]{0,2,1:T(2,128)} %broadcast_select_fusion.1), calls=%async_computation.2 | async-start | bytes 32768 | tf_op jit(solution)/shard_map/all_to_all | solution.py:76
  18.8 1.2 copy-start.2
  24.6 11.3 %all-to-all-start = ((s32[128,16,2,4]{0,2,3,1:T(2,128)}), s32[128,16,2,4]{0,2,3,1:T(2,128)S(1)}, u32[]{:S(2)}, u32[]{:S(2)}) async-start(s32[128,16,2,4]{0,2,3,1:T(2,128)} %fusion.14), calls=%async_computation | async-start | bytes 131072 | tf_op jit(solution)/shard_map/all_to_all | solution.py:75
  30.1 9.5 %copy-start.4 = (bf16[128,512]{1,0:T(8,128)(2,1)S(1)}, bf16[128,512]{1,0:T(8,128)(2,1)}, u32[]{:S(2)}) copy-start(bf16[128,512]{1,0:T(8,128)(2,1)} %param.15) | copy-start | bytes 393220
  35.9 26.5 %all-to-all-start.1 = ((bf16[128,16,2,128]{3,0,2,1:T(8,128)(2,1)}), bf16[128,16,2,128]{3,0,2,1:T(8,128)(2,1)S(1)}, u32[]{:S(2)}, u32[]{:S(2)}) async-start(bf16[128,16,2,128]{3,0,2,1:T(8,128)(2,1)} %broadcast_select_fusion), calls=%async_computation.1 | async-start | bytes 2097152 | tf_op jit(solution)/shard_map/all_to_all | solution.py:74
  39.5 63.9 %reduce-scatter.2.cloned.1.call-start = ((), (), s32[]{:S(2)}) async-start(), calls=%async_computation.4 | async-start | bytes 1114112 | tf_op jit(solution)/shard_map/reduce_scatter | solution.py:80
  40.9 106.2 %all-reduce.5.cloned.1.call-start = ((), (), s32[]{:S(2)}) async-start(), calls=%async_computation.6 | async-start | bytes 2228224 | tf_op jit(solution)/shard_map/psum | solution.py:78
  73.2 73.9 %copy-start.5 = (u32[32]{0:T(128)S(1)}, u32[32]{0:T(128)}, u32[]{:S(2)}) copy-start(u32[32]{0:T(128)} %constant.132) | copy-start | bytes 388
  103.5 114.0 %all-gather.2.cloned.1.call-start = ((), (), s32[]{:S(2)}) async-start(), calls=%async_computation.5 | async-start | bytes 1114112 | tf_op jit(solution)/shard_map/all_gather | solution.py:85
  217.5 2.4 %copy-start.3 = (f32[512,512]{1,0:T(8,128)S(1)}, f32[512,512]{1,0:T(8,128)}, u32[]{:S(2)}) copy-start(f32[512,512]{1,0:T(8,128)} %all-gather.2.cloned.1.call-done) | copy-start | bytes 3145732
Sparse Core Ops, SparseCore 0:
  44.6 58.8 reduce-scatter.1
  106.4 40.6 all-reduce.4
  149.3 37.8 all-gather.1
where the time goes:
time: 228 us; the launch traced here: 227 us
  waiting for transfers between devices  103 us (45%)
  blocking collectives  68.2 us (30%)
  starting transfers between devices  15.5 us (7%)
  between operations  15.3 us (7%)
  matrix products  9.65 us (4%)
  local copies, waits for them, and re-layouts  8.8 us (4%)
  other arithmetic  7.24 us (3%)
    unnamed x2, blocking collectives  63.2 us
    psum x1, waiting for transfers between devices, per_device(): table_grad = lax.psum(partial_grad, 'grp')  43.6 us
    reduce_scatter x1, waiting for transfers between devices, per_device(): lax.psum_scatter(weight_term, 'dev', scatter_dimension=0, tiled=True)  30.2 us
    all_to_all x1, waiting for transfers between devices, per_device(): lax.all_to_all(send_grads, 'dev', split_axis=1, concat_axis=0, tiled=True)  21.3 us
    dot_general x4, matrix products, add_block(): jnp.dot(counts.astype(jnp.bfloat16), values, preferred_element_type=jnp.f...  8.36 us
    all_to_all x1, starting transfers between devices, per_device(): lax.all_to_all(send_exps, 'dev', split_axis=1, concat_axis=0, tiled=True)  7.39 us
    all_to_all x1, waiting for transfers between devices, per_device(): lax.all_to_all(send_rows, 'dev', split_axis=1, concat_axis=0, tiled=True)  5.76 us
    psum x1, blocking collectives, per_device(): dense_parts = lax.psum((dense_parts[0], dense_parts[1]), 'grp')  4.93 us
  transfers between devices with their start and end apart: 6, of which 5 were waited for; matrix products, arithmetic and copies ran while one was open for 8% of the time, Pallas kernels for 0%

commit v1 on v0

--- a/solution.py
+++ b/solution.py
@@ -71,7 +71,12 @@
     )
     bias_term = jnp.sum(dense_cot.astype(jnp.float32), axis=0)
     partial_grad = accumulate(
-        lax.all_to_all(send_grads, "dev", split_axis=1, concat_axis=0, tiled=True),
+        jnp.concatenate(
+            lax.all_to_all(
+                jnp.stack(jnp.split(send_grads, lax.axis_size("dev"), axis=1)), "dev", 0, 0
+            ),
+            axis=0,
+        ),
         lax.all_to_all(send_rows, "dev", split_axis=1, concat_axis=0, tiled=True),
         lax.all_to_all(send_exps, "dev", split_axis=1, concat_axis=0, tiled=True),
     )

time: 228 us -> 237 us (1.039)
  local copies, waits for them, and re-layouts: 8.8 us -> 18.4 us
    unnamed x19 -> x32, local copies, waits for them, and re-layouts: 4.8 us -> 13.7 us
  transfers between devices with their start and end apart: 6 -> 6, of which waited for: 5 -> 4; matrix products, arithmetic and copies ran while one was open for 8% -> 12% of each run, Pallas kernels for 0% -> 0%
where the time goes in v1:
time: 237 us
  waiting for transfers between devices  101 us (43%)
  blocking collectives  68.2 us (29%)
  local copies, waits for them, and re-layouts  18.4 us (8%)
  starting transfers between devices  17.2 us (7%)
  between operations  15.3 us (6%)
  matrix products  9.65 us (4%)
  other arithmetic  6.61 us (3%)
    unnamed x2, blocking collectives  63.2 us
    psum x1, waiting for transfers between devices, per_device(): table_grad = lax.psum(partial_grad, 'grp')  43.6 us
    reduce_scatter x1, waiting for transfers between devices, per_device(): lax.psum_scatter(weight_term, 'dev', scatter_dimension=0, tiled=True)  30.3 us
    all_to_all x1, waiting for transfers between devices, per_device(): lax.all_to_all(jnp.stack(jnp.split(send_grads, lax.axis_size('dev'), axis...  21.3 us
    unnamed x32, local copies, waits for them, and re-layouts  13.7 us
    dot_general x4, matrix products, add_block(): jnp.dot(counts.astype(jnp.bfloat16), values, preferred_element_type=jnp.f...  8.36 us
    all_to_all x1, starting transfers between devices, per_device(): lax.all_to_all(send_exps, 'dev', split_axis=1, concat_axis=0, tiled=True)  7.39 us
    all_to_all x1, waiting for transfers between devices, per_device(): lax.all_to_all(send_rows, 'dev', split_axis=1, concat_axis=0, tiled=True)  6.26 us
  transfers between devices with their start and end apart: 6, of which 4 were waited for; matrix products, arithmetic and copies ran while one was open for 12% of the time, Pallas kernels for 0%

profile of v1, /device:TPU:0, one launch (start us, length us, event | category | flops | bytes accessed | tf_op | source)
XLA Modules:
  0.0 236.8 jit_solution(3204832119174360097)
XLA Ops:
  7.2 0.0 copy-start
  7.2 0.7 compare_select_fusion.5
  7.9 0.7 scatter_custom_fusion
  8.6 0.1 broadcast_in_dim.41
  8.7 1.3 gather_fusion.2
  10.0 0.7 broadcast_select_fusion.1
  10.7 7.4 %all-to-all-start.2 = ((s32[128,16,2]{0,2,1:T(2,128)}), s32[128,16,2]{0,2,1:T(2,128)S(1)}, u32[]{:S(2)}, u32[]{:S(2)}) async-start(s32[128,16,2]{0,2,1:T(2,128)} %broadcast_select_fusion.1), calls=%async_computation.2 | async-start | bytes 32768 | tf_op jit(solution)/shard_map/all_to_all | solution.py:81
  18.1 0.7 select_add_fusion
  18.8 1.8 clamp_convert_fusion
  20.6 0.7 gather_fusion.1
  21.3 0.2 broadcast_select_fusion
  21.5 0.0 copy-start.1
  21.5 0.6 fusion.29
  22.1 0.6 fusion.28
  22.8 0.6 fusion.27
  23.4 0.6 fusion.26
  24.1 0.6 fusion.25
  24.7 0.6 fusion.24
  25.3 0.6 fusion.23
  26.0 0.6 fusion.22
  26.6 0.6 fusion.21
  27.2 0.6 fusion.20
  27.9 0.6 fusion.19
  28.5 0.6 fusion.18
  29.1 0.6 fusion.17
  29.8 0.6 fusion.16
  30.4 0.6 gather_fusion
  31.0 0.7 fusion.30
  31.8 0.6 fusion.15
  32.4 6.0 %all-to-all-start = ((s32[128,16,2,4]{0,2,3,1:T(2,128)}), s32[128,16,2,4]{0,2,3,1:T(2,128)S(1)}, u32[]{:S(2)}, u32[]{:S(2)}) async-start(s32[128,16,2,4]{0,2,3,1:T(2,128)} %fusion.30), calls=%async_computation | async-start | bytes 131072 | tf_op jit(solution)/shard_map/all_to_all | solution.py:80
  38.4 0.6 fusion.14
  39.1 6.3 %all-to-all-done = s32[128,16,2,4]{0,2,3,1:T(2,128)S(1)} async-done(((s32[128,16,2,4]{0,2,3,1:T(2,128)}), s32[128,16,2,4]{0,2,3,1:T(2,128)S(1)}, u32[]{:S(2)}, u32[]{:S(2)}) %all-to-all-start) | async-done | bytes 65568 | tf_op jit(solution)/shard_map/all_to_all | solution.py:80
  45.3 3.7 %all-to-all-start.1 = ((bf16[16,128,1,2,128]{4,1,3,2,0:T(8,128)(2,1)}), bf16[16,128,1,2,128]{4,1,3,2,0:T(8,128)(2,1)S(1)}, u32[]{:S(2)}, u32[]{:S(2)}) async-start(bf16[16,128,1,2,128]{4,1,3,2,0:T(8,128)(2,1)} %fusion.14), calls=%async_computation.1 | async-start | bytes 2097152 | tf_op jit(solution)/shard_map/all_to_all | solution.py:75
  49.0 0.0 reduce-scatter.2.cloned.1.call-start
  49.1 1.3 fusion.41
  50.3 0.0 reduce-scatter.2.cloned.1.call-update
  50.4 0.0 all-reduce.5.cloned.1.call-start
  50.6 21.3 %all-to-all-done.1 = bf16[16,128,1,2,128]{4,1,3,2,0:T(8,128)(2,1)S(1)} async-done(((bf16[16,128,1,2,128]{4,1,3,2,0:T(8,128)(2,1)}), bf16[16,128,1,2,128]{4,1,3,2,0:T(8,128)(2,1)S(1)}, u32[]{:S(2)}, u32[]{:S(2)}) %all-to-all-start.1) | async-done | bytes 1048608 | tf_op jit(solution)/shard_map/all_to_all | solution.py:75
  71.8 0.1 copy.40
  71.9 0.7 fusion.13
  72.7 4.5 %while.30 = (s32[]{:T(128)}, f32[1024,128]{1,0:T(8,128)S(1)}, s32[2048,4]{0,1:T(4,128)S(1)}, bf16[2048,128]{1,0:T(8,128)(2,1)S(1)}, s32[]{:T(128)}, /*index=5*/s...) while((s32[]{:T(128)}, f32[1024,128]{1,0:T(8,128)S(1)}, ...), condition=%wide.region_2.3_spmd.clone.clone, body=%wide.region_1.2_spmd.clone.clone.sunk | while | flops 281280512 | bytes 1360093 | solution.py:45
  72.7 0.1 constant_dynamic-slice_fusion.4
  72.8 2.1 fusion.49
  74.9 0.1 constant_dynamic-slice_fusion.4
  75.0 2.1 fusion.49
  77.1 4.5 %while.31 = (s32[]{:T(128)}, f32[1024,128]{1,0:T(8,128)S(1)}, s32[2048,4]{0,1:T(4,128)S(1)}, bf16[2048,128]{1,0:T(8,128)(2,1)S(1)}, s32[]{:T(128)}, /*index=5*/s...) while((s32[]{:T(128)}, f32[1024,128]{1,0:T(8,128)S(1)}, ...), condition=%wide.region_4.5_spmd.clone.clone, body=%wide.region_3.4_spmd.clone.clone.sunk | while | flops 281280512 | bytes 1360093 | solution.py:45
  77.1 0.1 constant_dynamic-slice_fusion.5
  77.3 2.1 fusion.51
  79.4 0.1 constant_dynamic-slice_fusion.5
  79.5 2.1 fusion.51
  81.6 1.0 pad_maximum_fusion
  82.6 30.3 %reduce-scatter.2.cloned.1.call-done = f32[32,512]{1,0:T(8,128)} async-done(((f32[512,512]{1,0:T(8,128)}), f32[32,512]{1,0:T(8,128)}) %reduce-scatter.2.cloned.1.call-update) | async-done | bytes 65552 | tf_op jit(solution)/shard_map/reduce_scatter | solution.py:85
  112.9 0.0 all-reduce.5.cloned.1.call-update
  112.9 0.0 all-gather.2.cloned.1.call-start
  113.0 43.6 %all-reduce.5.cloned.1.call-done = (f32[2,1024,128]{2,1,0:T(8,128)}, f32[32,512]{1,0:T(8,128)}) async-done(((f32[2,1024,128]{2,1,0:T(8,128)}, f32[32,512]{1,0:T(8,128)}), (f32[2,1024,128]{2,1,0:T(8,128)}, f32[32,512]{1,0:T(8,128)})) %all-reduce.5.cloned.1.call-update) | async-done | bytes 1114128 | tf_op jit(solution)/shard_map/psum | solution.py:83
  156.5 0.0 all-gather.2.cloned.1.call-update
  156.6 0.6 fusion.40
  157.8 33.2 %all-reduce.1 = f32[512]{0:T(512)S(1)} all-reduce(f32[512]{0:T(512)S(1)} %convert_reduce_fusion), channel_id=3, replica_groups=mesh['grp'=2,'dev'=16] {'dev'}, use_global_device_ids=true, to_apply=%region_9.10.clone | all-reduce | flops 512 | bytes 4096
  191.0 0.1 dynamic-slice.2
  191.8 4.9 %psum.23 = f32[32]{0:T(128)S(1)} all-reduce(f32[32]{0:T(128)S(1)} %dynamic-slice.2), channel_id=1, replica_groups=mesh['grp'=2,'dev'=16] {'grp'}, use_global_device_ids=true, to_apply=%region_10.11 | all-reduce | flops 32 | bytes 256 | tf_op jit(solution)/shard_map/psum | solution.py:88
  196.7 0.2 dynamic-update-slice
  196.9 30.0 %all-reduce = f32[512]{0:T(512)} all-reduce(f32[512]{0:T(512)S(1)} %dynamic-update-slice), channel_id=1, replica_groups=mesh['grp'=2,'dev'=16] {'dev'}, use_global_device_ids=true, to_apply=%add | all-reduce | flops 512 | bytes 4096
  226.9 2.4 copy.81
  229.3 1.0 copy.82
  (23 shorter events, 0.2 us)
Async XLA Ops:
  7.2 41.9 %copy-start = (bf16[128,512]{1,0:T(8,128)(2,1)S(1)}, bf16[128,512]{1,0:T(8,128)(2,1)}, u32[]{:S(2)}) copy-start(bf16[128,512]{1,0:T(8,128)(2,1)} %param.14) | copy-start | bytes 393220
  10.7 21.7 %all-to-all-start.2 = ((s32[128,16,2]{0,2,1:T(2,128)}), s32[128,16,2]{0,2,1:T(2,128)S(1)}, u32[]{:S(2)}, u32[]{:S(2)}) async-start(s32[128,16,2]{0,2,1:T(2,128)} %broadcast_select_fusion.1), calls=%async_computation.2 | async-start | bytes 32768 | tf_op jit(solution)/shard_map/all_to_all | solution.py:81
  21.5 8.9 %copy-start.1 = (s32[128,4,32]{0,2,1:T(8,128)S(1)}, s32[128,4,32]{0,2,1:T(8,128)}, u32[]{:S(2)}) copy-start(s32[128,4,32]{0,2,1:T(8,128)} %param.11) | copy-start | bytes 196612
  32.4 12.9 %all-to-all-start = ((s32[128,16,2,4]{0,2,3,1:T(2,128)}), s32[128,16,2,4]{0,2,3,1:T(2,128)S(1)}, u32[]{:S(2)}, u32[]{:S(2)}) async-start(s32[128,16,2,4]{0,2,3,1:T(2,128)} %fusion.30), calls=%async_computation | async-start | bytes 131072 | tf_op jit(solution)/shard_map/all_to_all | solution.py:80
  39.1 10.0 %copy-start.3 = (bf16[128,512]{1,0:T(8,128)(2,1)S(1)}, bf16[128,512]{1,0:T(8,128)(2,1)}, u32[]{:S(2)}) copy-start(bf16[128,512]{1,0:T(8,128)(2,1)} %param.15) | copy-start | bytes 393220
  45.3 26.5 %all-to-all-start.1 = ((bf16[16,128,1,2,128]{4,1,3,2,0:T(8,128)(2,1)}), bf16[16,128,1,2,128]{4,1,3,2,0:T(8,128)(2,1)S(1)}, u32[]{:S(2)}, u32[]{:S(2)}) async-start(bf16[16,128,1,2,128]{4,1,3,2,0:T(8,128)(2,1)} %fusion.14), calls=%async_computation.1 | async-start | bytes 2097152 | tf_op jit(solution)/shard_map/all_to_all | solution.py:75
  49.0 63.9 %reduce-scatter.2.cloned.1.call-start = ((), (), s32[]{:S(2)}) async-start(), calls=%async_computation.4 | async-start | bytes 1114112 | tf_op jit(solution)/shard_map/reduce_scatter | solution.py:85
  50.4 106.2 %all-reduce.5.cloned.1.call-start = ((), (), s32[]{:S(2)}) async-start(), calls=%async_computation.6 | async-start | bytes 2228224 | tf_op jit(solution)/shard_map/psum | solution.py:83
  82.6 73.9 %copy-start.4 = (u32[32]{0:T(128)S(1)}, u32[32]{0:T(128)}, u32[]{:S(2)}) copy-start(u32[32]{0:T(128)} %constant.132) | copy-start | bytes 388
  112.9 114.0 %all-gather.2.cloned.1.call-start = ((), (), s32[]{:S(2)}) async-start(), calls=%async_computation.5 | async-start | bytes 1114112 | tf_op jit(solution)/shard_map/all_gather | solution.py:90
  226.9 2.4 copy-start.2
Sparse Core Ops, SparseCore 0:
  54.0 58.8 reduce-scatter.1
  115.9 40.6 all-reduce.4
  158.7 37.8 all-gather.1
